TPU v7x, 32 devices: a whole 2x2x4 slice. The times are simulated.
32 devices in a mesh: dp: 32 (over z, y, x, core).
Axes of the slice: x: 2, y: 2, z: 4, core: 2. Of those that a mesh axis runs over, the one named last changes fastest.
Arguments:
- features: bfloat16 [256, 128, 1024], P('dp'), may hold values from -16 to 16
- ln_gain: float32 [1024], replicated, may hold values from 0.5 to 1.5
- w_query: bfloat16 [1024, 1024], replicated, may hold values from -0.1875 to 0.1875
- w_key: bfloat16 [1024, 1024], replicated, may hold values from -0.1875 to 0.1875
- w_value: bfloat16 [1024, 1024], replicated, may hold values from -0.1875 to 0.1875
- w_out: bfloat16 [1024, 1024], replicated, may hold values from -0.1875 to 0.1875
- text_raw: bfloat16 [256, 1024], P('dp'), may hold values from -0.35 to 0.35
Outputs:
- loss: float32 [], replicated
- text_grad: float32 [256, 1024], P('dp')
- w_out_grad: bfloat16 [1024, 1024], replicated
All inputs are finite; a program needn't handle non-finite values.
Results may differ from a plain program's by a relative error of at most 0.009.
Values may be sent and summed in bfloat16 or wider, within the bound.
No kernel may reach another device: no remote copies, remote signals or barrier semaphores. Data moves between devices by JAX's collectives and lax.ppermute only.
A program may use at most 128 MiB of HBM per device.

v0:
```python
import jax
import jax.numpy as jnp
from jax import lax
from jax.sharding import PartitionSpec as P

HEADS = 16
inv_temp = 1.0 / 0.07
attn_temp = 8.0
epsilon = 1e-06


def layer_norm(inputs, gain):
    center = inputs - jnp.mean(inputs, axis=-1, keepdims=True)
    spread = jnp.mean(center * center, axis=-1, keepdims=True)
    return center * lax.rsqrt(spread + epsilon) * gain


def unit_heads(proj, heads):
    shaped = proj.reshape(proj.shape[0], proj.shape[1], heads, -1)
    return (shaped * lax.rsqrt(jnp.sum(shaped * shaped, axis=-1, keepdims=True) + epsilon)).astype(
        jnp.bfloat16
    )


def embed(feats, ln_gain, w_query, w_key, w_value, w_out):
    images, tokens, width = feats.shape
    inputs = feats.astype(jnp.float32)
    normed = layer_norm(inputs, ln_gain).astype(jnp.bfloat16).reshape(images * tokens, width)
    query = unit_heads(
        jnp.dot(normed, w_query, preferred_element_type=jnp.float32).reshape(images, tokens, width),
        HEADS,
    )
    key_heads = unit_heads(
        jnp.dot(normed, w_key, preferred_element_type=jnp.float32).reshape(images, tokens, width),
        HEADS,
    )
    value_heads = (
        jnp.dot(normed, w_value, preferred_element_type=jnp.float32)
        .reshape(images, tokens, HEADS, -1)
        .astype(jnp.bfloat16)
    )
    scores = attn_temp * jnp.einsum(
        "bqhd,bkhd->bhqk", query, key_heads, preferred_element_type=jnp.float32
    )
    expo = jnp.exp(scores)
    weights = (
        (expo / jnp.sum(expo, axis=-1, keepdims=True)).astype(jnp.bfloat16).astype(jnp.float32)
    )
    pooled = weights[:, :, 0, :] + jnp.mean(weights[:, :, 1:, :], axis=2)
    abar = jnp.einsum(
        "bhk,bkhd->bhd", pooled, value_heads.astype(jnp.float32), precision=lax.Precision.HIGHEST
    )
    abar = abar.reshape(images, width).astype(jnp.bfloat16)
    xbar = inputs[:, 0, :] + jnp.mean(inputs[:, 1:, :], axis=1)
    emb = xbar + jnp.dot(abar, w_out, preferred_element_type=jnp.float32)
    return (emb, abar)


def local(features, ln_gain, w_query, w_key, w_value, w_out, text_raw):
    images = features.shape[0]
    total = images * lax.axis_size("dp")
    offset = lax.axis_index("dp") * images
    text32 = text_raw.astype(jnp.float32)
    txt_norm = jnp.sqrt(jnp.sum(text32 * text32, axis=1, keepdims=True) + epsilon)
    txt_f = text32 / txt_norm
    txt_u = txt_f.astype(jnp.bfloat16)
    emb, abar = embed(features, ln_gain, w_query, w_key, w_value, w_out)
    emb_norm = jnp.sqrt(jnp.sum(emb * emb, axis=1, keepdims=True) + epsilon)
    img_f = emb / emb_norm
    img_u = img_f.astype(jnp.bfloat16)
    row_index = lax.broadcasted_iota(jnp.int32, (images, total), 0)
    col_index = lax.broadcasted_iota(jnp.int32, (images, total), 1)
    diag_mask = jnp.where(col_index == row_index + offset, 1.0, 0.0).astype(jnp.float32)
    all_img, all_txt = (
        lax.all_gather(img_u, "dp", axis=0, tiled=True),
        lax.all_gather(txt_u, "dp", axis=0, tiled=True),
    )
    logits = inv_temp * jnp.dot(all_img, all_txt.T, preferred_element_type=jnp.float32)
    exp_logits = jnp.exp(logits)
    rowsum = jnp.sum(exp_logits, axis=1)
    colsum = jnp.sum(exp_logits, axis=0)
    diag_logit = jnp.diagonal(logits)
    loss = (jnp.sum(jnp.log(rowsum) - diag_logit) + jnp.sum(jnp.log(colsum) - diag_logit)) / (
        2.0 * total
    )
    row_block = lax.dynamic_slice_in_dim(exp_logits, offset, images, 0)
    own_rowsum = lax.dynamic_slice_in_dim(rowsum, offset, images, 0)
    delta_rows = 0.5 * (row_block / own_rowsum[:, None] + row_block / colsum[None, :]) - diag_mask
    delta_rows = delta_rows.astype(jnp.bfloat16)
    col_block = lax.dynamic_slice_in_dim(exp_logits, offset, images, 1)
    own_colsum = lax.dynamic_slice_in_dim(colsum, offset, images, 0)
    delta_cols = 0.5 * (col_block / rowsum[:, None] + col_block / own_colsum[None, :]) - diag_mask.T
    delta_cols = delta_cols.astype(jnp.bfloat16)
    grad_img = inv_temp * jnp.dot(delta_rows, all_txt, preferred_element_type=jnp.float32)
    grad_txt = inv_temp * lax.dot_general(
        delta_cols, all_img, (((0,), (0,)), ((), ())), preferred_element_type=jnp.float32
    )
    text_grad = (grad_txt - txt_f * jnp.sum(txt_f * grad_txt, axis=1, keepdims=True)) / txt_norm
    emb_grad = (grad_img - img_f * jnp.sum(img_f * grad_img, axis=1, keepdims=True)) / emb_norm
    local_grad = jnp.dot(abar.astype(jnp.float32).T, emb_grad, precision=lax.Precision.HIGHEST)
    w_out_grad = lax.psum(local_grad, "dp").astype(jnp.bfloat16)
    return (loss, text_grad, w_out_grad)


def solution(mesh):
    placed = (P("dp", None, None), P(), P(), P(), P(), P(), P("dp", None))
    return jax.shard_map(
        local, mesh=mesh, in_specs=placed, out_specs=(P(), P("dp", None), P()), check_vma=False
    )
```

profile of v0, /device:TPU:0, one launch (start us, length us, event | category | flops | bytes accessed | tf_op | source)
XLA Modules:
  0.0 256.5 jit_solution(18150039622632288894)
XLA Ops:
  0.7 2.9 %convert_reduce_fusion = f32[8,128]{0,1:T(8,128)S(1)} fusion(bf16[8,128,1024]{2,1,0:T(8,128)(2,1)} %param.7), kind=kLoop, calls=%fused_computation.16 | loop fusion | flops 2096128 | bytes 2101248 | tf_op jit(solution)/shard_map/reduce_sum | solution.py:13
  3.6 2.9 %multiply_reduce_fusion.2 = f32[8,128]{0,1:T(8,128)S(1)} fusion(f32[8,128]{0,1:T(8,128)S(1)} %broadcast_multiply_fusion, bf16[8,128,1024]{2,1,0:T(8,128)(2,1)} %param.7), kind=kLoop, calls=%fused_computation.14 | loop fusion | flops 4193280 | bytes 2105344 | tf_op jit(solution)/shard_map/reduce_sum | solution.py:14
  6.5 2.7 %fusion.14 = bf16[8,128,1024,1]{2,0,1,3:T(8,128)(2,1)} fusion(f32[1024]{0:T(1024)S(1)} %copy-done.4, f32[8,128]{0,1:T(8,128)S(1)} %add_rsqrt_fusion.2, f32[8,128]{0,1:T(8,128)S(1)} %broadcast_multiply_fusion, bf16[8,128,1024]{2,1,0:T(8,128)(2,1)S(1)} %copy-done.1), kind=kLoop, calls=%fused_computation.32 | loop fusion | flops 5242880 | bytes 4206592 | tf_op jit(solution)/shard_map/convert_element_type | solution.py:28
  9.2 3.9 %copy.38 = bf16[1024,1024]{0,1:T(8,128)(2,1)} copy(bf16[1024,1024]{1,0:T(8,128)(2,1)} %param.10) | data formatting | bytes 4194304 | tf_op args[3]
  13.1 7.6 %multiply_reduce_fusion = (f32[8,128,16]{1,2,0:T(8,128)S(1)}, f32[8,128,16,64]{1,3,2,0:T(8,128)}) fusion(bf16[16,64,1024,1]{2,1,0,3:T(8,128)(2,1)} %bitcast.49, bf16[8,128,1024,1]{2,0,1,3:T(8,128)(2,1)} %fusion.14), kind=kOutput, calls=%fused_computation.10 | convolution fusion | flops 2149564416 | bytes 8454144 | tf_op jit(solution)/shard_map/dot_general | solution.py:34
  20.7 3.9 %copy.36 = bf16[1024,1024]{0,1:T(8,128)(2,1)} copy(bf16[1024,1024]{1,0:T(8,128)(2,1)} %param.9) | data formatting | bytes 4194304 | tf_op args[2]
  24.6 5.8 %multiply_reduce_fusion.1 = (f32[8,128,16]{1,2,0:T(8,128)S(1)}, f32[8,128,16,64]{1,3,2,0:T(8,128)S(1)}) fusion(bf16[16,64,1024,1]{2,1,0,3:T(8,128)(2,1)} %bitcast.48, bf16[8,128,1024,1]{2,0,1,3:T(8,128)(2,1)} %fusion.14), kind=kOutput, calls=%fused_computation.12 | convolution fusion | flops 2149564416 | bytes 8454144 | tf_op jit(solution)/shard_map/dot_general | solution.py:30
  30.4 1.3 fusion.6
  31.8 15.0 %fusion.5 = f32[8,16,128,128]{3,2,1,0:T(8,128)S(1)} fusion(f32[8,16,128,128]{3,2,1,0:T(8,128)S(1)} %fusion.6), kind=kOutput, calls=%fused_computation.17 | output fusion | flops 10502271 | bytes 16777216 | tf_op jit(solution)/shard_map/div | solution.py:47
  46.9 1.9 slice_reduce_fusion
  48.9 3.9 %copy.40 = bf16[1024,1024]{0,1:T(8,128)(2,1)} copy(bf16[1024,1024]{1,0:T(8,128)(2,1)} %param.11) | data formatting | bytes 4194304 | tf_op args[4]
  52.8 7.5 %convolution_convert_fusion = bf16[8,128,16,64]{3,0,2,1:T(8,128)(2,1)S(1)} fusion(bf16[16,64,1024,1]{2,1,0,3:T(8,128)(2,1)} %bitcast.50, f32[1024]{0:T(1024)S(1)} %copy-done.4, f32[8,128]{0,1:T(8,128)S(1)} %add_rsqrt_fusion.2, f32[8,128]{0,1:T(8,128)S(1)} %broadcast_multiply_fusion, bf16[8,128,1024]{2,1,0:T(8,128)(2,1)} %param.7), kind=kOutput, calls=%fused_computation.18 | convolution fusion | flops 2153775104 | bytes 6303744 | tf_op jit(solution)/shard_map/dot_general | solution.py:38
  60.3 7.0 %fusion.2 = f32[8,16,1,64]{3,2,1,0:T(1,128)S(1)} fusion(f32[8,16,128,1]{2,3,1,0:T(1,128)S(1)} %bitcast.51, bf16[8,128,16,64]{3,0,2,1:T(8,128)(2,1)S(1)} %convolution_convert_fusion), kind=kOutput, calls=%fused_computation.6 | convolution fusion | flops 12582912 | bytes 2195456 | tf_op jit(solution)/shard_map/bhk,bkhd->bhd/dot_general | solution.py:50
  67.3 0.1 convert_element_type.55
  67.4 2.8 %copy_convert_fusion = f32[8,128,1024]{2,0,1:T(8,128)S(1)} fusion(bf16[8,128,1024]{2,1,0:T(8,128)(2,1)} %param.7), kind=kLoop, calls=%fused_computation.27 | loop fusion | flops 1048576 | bytes 6291456 | tf_op jit(solution)/shard_map/convert_element_type | solution.py:27
  70.2 0.3 slice_reduce_fusion.1
  70.5 0.5 multiply_reduce_fusion.5
  71.0 0.1 fusion.45
  71.1 44.7 %all_gather.6 = bf16[256,1024]{1,0:T(8,128)(2,1)S(1)} all-gather(bf16[8,1024]{1,0:T(8,128)(2,1)S(1)} %fusion.45), channel_id=1, replica_groups=mesh['dp'=32] {'dp'}, dimensions={0}, use_global_device_ids=true | all-gather | bytes 540672 | tf_op jit(solution)/shard_map/all_gather | solution.py:75
  115.8 0.1 fusion.21
  115.9 0.1 fusion.44
  116.0 38.3 %all_gather.7 = bf16[256,1024]{1,0:T(8,128)(2,1)S(1)} all-gather(bf16[8,1024]{1,0:T(8,128)(2,1)S(1)} %fusion.44), channel_id=1, replica_groups=mesh['dp'=32] {'dp'}, dimensions={0}, use_global_device_ids=true | all-gather | bytes 540672 | tf_op jit(solution)/shard_map/all_gather | solution.py:76
  154.3 1.0 exponential_reduce_fusion
  155.3 0.1 dynamic_slice.15
  155.4 1.3 multiply_reduce_fusion.3
  156.8 3.8 %fusion.23 = f32[1024,1024]{1,0:T(8,128)} fusion(bf16[8,1024]{1,0:T(8,128)(2,1)S(1)} %convert_element_type.55, f32[8,1024]{1,0:T(8,128)S(1)} %get-tuple-element.18, f32[8]{0:T(128)S(1)} %get-tuple-element.17, f32[8]{0:T(128)S(1)} %add_sqrt_fusion.1, f32[8,1024]{1,0:T(8,128)S(1)} %get-tuple-element.13), kind=kOutput, calls=%fused_computation.50 | convolution fusion | flops 100696064 | bytes 4276288 | tf_op jit(solution)/shard_map/dot_general | solution.py:100
  160.5 88.6 %all-reduce.1 = bf16[1024,1024]{1,0:T(8,128)(2,1)} all-reduce(f32[1024,1024]{1,0:T(8,128)} %fusion.23), channel_id=1, replica_groups=mesh['dp'=32] {'dp'}, use_global_device_ids=true, to_apply=%region_15.16 | all-reduce | flops 1048576 | bytes 6291456 | tf_op jit(solution)/shard_map/psum | solution.py:101
  249.2 0.1 dynamic_slice.13
  249.2 1.0 multiply_reduce_fusion.4
  250.3 0.7 subtract_divide_fusion
  251.0 2.4 gather_fusion
  253.4 0.7 subtract_reduce_fusion
  (20 shorter events, 0.2 us)
Async XLA Ops:
  0.6 69.9 %copy-start = (bf16[1024,1024]{1,0:T(8,128)(2,1)S(1)}, bf16[1024,1024]{1,0:T(8,128)(2,1)}, u32[]{:S(2)}) copy-start(bf16[1024,1024]{1,0:T(8,128)(2,1)} %param.12) | copy-start | bytes 6291460
  0.6 5.8 %copy-start.1 = (bf16[8,128,1024]{2,1,0:T(8,128)(2,1)S(1)}, bf16[8,128,1024]{2,1,0:T(8,128)(2,1)}, u32[]{:S(2)}) copy-start(bf16[8,128,1024]{2,1,0:T(8,128)(2,1)} %param.7) | copy-start | bytes 6291460
  0.7 5.8 %copy-start.4 = (f32[1024]{0:T(1024)S(1)}, f32[1024]{0:T(1024)}, u32[]{:S(2)}) copy-start(f32[1024]{0:T(1024)} %param.8) | copy-start | bytes 12292
  24.6 5.8 %copy-start.2 = (f32[8,128,16,64]{1,3,2,0:T(8,128)S(1)}, f32[8,128,16,64]{1,3,2,0:T(8,128)}, u32[]{:S(2)}) copy-start(f32[8,128,16,64]{1,3,2,0:T(8,128)} %get-tuple-element.9) | copy-start | bytes 12582916
  70.2 45.6 %copy-start.3 = (bf16[8,1024]{1,0:T(8,128)(2,1)S(1)}, bf16[8,1024]{1,0:T(8,128)(2,1)}, u32[]{:S(2)}) copy-start(bf16[8,1024]{1,0:T(8,128)(2,1)} %param.13) | copy-start | bytes 49156
where the time goes:
time: 257 us
  blocking collectives  172 us (67%)
  matrix products  36.8 us (14%)
  other arithmetic  30.3 us (12%)
  local copies, waits for them, and re-layouts  14.5 us (6%)
  between operations  3.26 us (1%)
    psum x1, blocking collectives, local(): w_out_grad = lax.psum(local_grad, 'dp').astype(jnp.bfloat16)  88.6 us
    all_gather x1, blocking collectives, local(): lax.all_gather(img_u, 'dp', axis=0, tiled=True)  44.7 us
    all_gather x1, blocking collectives, local(): lax.all_gather(txt_u, 'dp', axis=0, tiled=True)  38.3 us
    div x1, other arithmetic, embed(): expo / jnp.sum(expo, axis=-1, keepdims=True)  15 us
    unnamed x13, local copies, waits for them, and re-layouts  11.8 us
    dot_general x1, matrix products, embed(): jnp.dot(normed, w_key, preferred_element_type=jnp.float32)  7.56 us
    dot_general x1, matrix products, embed(): jnp.dot(normed, w_value, preferred_element_type=jnp.float32)  7.53 us
    dot_general x1, matrix products, embed(): jnp.einsum('bhk,bkhd->bhd', pooled, value_heads.astype(jnp.float32), prec...  6.95 us

commit v1 on v0

--- a/solution.py
+++ b/solution.py
@@ -73,7 +73,9 @@
     diag_mask = jnp.where(col_index == row_index + offset, 1.0, 0.0).astype(jnp.float32)
     all_img, all_txt = (
         lax.all_gather(img_u, "dp", axis=0, tiled=True),
-        lax.all_gather(txt_u, "dp", axis=0, tiled=True),
+        jnp.concatenate(
+            lax.all_to_all(jnp.stack([txt_u] * lax.axis_size("dp")), "dp", 0, 0), axis=0
+        ),
     )
     logits = inv_temp * jnp.dot(all_img, all_txt.T, preferred_element_type=jnp.float32)
     exp_logits = jnp.exp(logits)

time: 257 us -> 226 us (0.88)
  blocking collectives: 172 us -> 132 us
  starting transfers between devices: 0 us -> 7.33 us
    all_gather x1 -> x0, blocking collectives: 38.3 us -> none  [local(): lax.all_gather(txt_u, 'dp', axis=0, tiled=True)]
    all_to_all x0 -> x1, starting transfers between devices: none -> 7.33 us  [local(): lax.all_to_all(jnp.stack([txt_u] * lax.axis_size('dp')), 'dp', 0, 0)]
    dot_general x1, matrix products: 7.56 us -> 3.49 us  [embed(): jnp.dot(normed, w_key, preferred_element_type=jnp.float32)]
    dot_general x1, matrix products: 6.95 us -> 10 us  [embed(): jnp.einsum('bhk,bkhd->bhd', pooled, value_heads.astype(jnp.float32), prec...]
    unnamed x13 -> x19, local copies, waits for them, and re-layouts: 11.8 us -> 12 us
  transfers between devices with their start and end apart: 0 -> 1, of which waited for: 0 -> 0; matrix products, arithmetic and copies ran while one was open for 0% -> 31% of each run, Pallas kernels for 0% -> 0%
where the time goes in v1:
time: 226 us; the launch traced here: 225 us
  blocking collectives  132 us (58%)
  matrix products  34.3 us (15%)
  other arithmetic  32.7 us (14%)
  local copies, waits for them, and re-layouts  15.6 us (7%)
  starting transfers between devices  7.33 us (3%)
  between operations  3.3 us (1%)
    psum x1, blocking collectives, local(): w_out_grad = lax.psum(local_grad, 'dp').astype(jnp.bfloat16)  88.3 us
    all_gather x1, blocking collectives, local(): lax.all_gather(img_u, 'dp', axis=0, tiled=True)  43.4 us
    div x1, other arithmetic, embed(): expo / jnp.sum(expo, axis=-1, keepdims=True)  15.3 us
    unnamed x19, local copies, waits for them, and re-layouts  12 us
    dot_general x1, matrix products, embed(): jnp.einsum('bhk,bkhd->bhd', pooled, value_heads.astype(jnp.float32), prec...  10 us
    dot_general x1, matrix products, embed(): jnp.dot(normed, w_value, preferred_element_type=jnp.float32)  9.04 us
    all_to_all x1, starting transfers between devices, local(): lax.all_to_all(jnp.stack([txt_u] * lax.axis_size('dp')), 'dp', 0, 0)  7.33 us
  transfers between devices with their start and end apart: 1, of which 0 were waited for; matrix products, arithmetic and copies ran while one was open for 31% of the time, Pallas kernels for 0%

profile of v1, /device:TPU:0, one launch (start us, length us, event | category | flops | bytes accessed | tf_op | source)
XLA Modules:
  0.0 224.9 jit_solution(16333641841021918606)
XLA Ops:
  0.6 1.0 fusion.23
  1.6 0.8 fusion.46
  2.4 0.9 stack.2
  3.4 7.3 %all-to-all-start = ((bf16[32,8,1024]{2,1,0:T(8,128)(2,1)}), bf16[32,8,1024]{2,1,0:T(8,128)(2,1)S(1)}, u32[]{:S(2)}, u32[]{:S(2)}) async-start(bf16[32,8,1024]{2,1,0:T(8,128)(2,1)} %stack.2), calls=%async_computation | async-start | bytes 1048576 | tf_op jit(solution)/shard_map/all_to_all | solution.py:77
  10.7 2.8 %convert_reduce_fusion = f32[8,128]{0,1:T(8,128)S(1)} fusion(bf16[8,128,1024]{2,1,0:T(8,128)(2,1)} %param.7), kind=kLoop, calls=%fused_computation.16 | loop fusion | flops 2096128 | bytes 2101248 | tf_op jit(solution)/shard_map/reduce_sum | solution.py:13
  13.5 2.9 %multiply_reduce_fusion.2 = f32[8,128]{0,1:T(8,128)S(1)} fusion(f32[8,128]{0,1:T(8,128)S(1)} %broadcast_multiply_fusion, bf16[8,128,1024]{2,1,0:T(8,128)(2,1)} %param.7), kind=kLoop, calls=%fused_computation.14 | loop fusion | flops 4193280 | bytes 2105344 | tf_op jit(solution)/shard_map/reduce_sum | solution.py:14
  16.4 4.0 %copy.38 = bf16[1024,1024]{0,1:T(8,128)(2,1)} copy(bf16[1024,1024]{1,0:T(8,128)(2,1)} %param.10) | data formatting | bytes 4194304 | tf_op args[3]
  20.3 3.9 %copy.36 = bf16[1024,1024]{0,1:T(8,128)(2,1)} copy(bf16[1024,1024]{1,0:T(8,128)(2,1)} %param.9) | data formatting | bytes 4194304 | tf_op args[2]
  24.3 3.1 %fusion.14 = bf16[8,128,1024,1]{2,0,1,3:T(8,128)(2,1)S(1)} fusion(f32[1024]{0:T(1024)S(1)} %copy-done.7, f32[8,128]{0,1:T(8,128)S(1)} %add_rsqrt_fusion.2, f32[8,128]{0,1:T(8,128)S(1)} %broadcast_multiply_fusion, bf16[8,128,1024]{2,1,0:T(8,128)(2,1)} %param.7), kind=kLoop, calls=%fused_computation.32 | loop fusion | flops 5242880 | bytes 4206592 | tf_op jit(solution)/shard_map/convert_element_type | solution.py:28
  27.4 3.5 %multiply_reduce_fusion = (f32[8,128,16]{1,2,0:T(8,128)S(1)}, f32[8,128,16,64]{1,3,2,0:T(8,128)S(1)}) fusion(bf16[16,64,1024,1]{2,1,0,3:T(8,128)(2,1)S(1)} %bitcast.56, bf16[8,128,1024,1]{2,0,1,3:T(8,128)(2,1)S(1)} %fusion.14), kind=kOutput, calls=%fused_computation.10 | convolution fusion | flops 2149564416 | bytes 8454144 | tf_op jit(solution)/shard_map/dot_general | solution.py:34
  30.9 3.5 %multiply_reduce_fusion.1 = (f32[8,128,16]{1,2,0:T(8,128)S(1)}, f32[8,128,16,64]{1,3,2,0:T(8,128)S(1)}) fusion(bf16[16,64,1024,1]{2,1,0,3:T(8,128)(2,1)S(1)} %bitcast.55, bf16[8,128,1024,1]{2,0,1,3:T(8,128)(2,1)S(1)} %fusion.14), kind=kOutput, calls=%fused_computation.12 | convolution fusion | flops 2149564416 | bytes 8454144 | tf_op jit(solution)/shard_map/dot_general | solution.py:30
  34.4 1.3 fusion.6
  35.7 15.3 %fusion.5 = f32[8,16,128,128]{3,2,1,0:T(8,128)S(1)} fusion(f32[8,16,128,128]{3,2,1,0:T(8,128)S(1)} %fusion.6), kind=kOutput, calls=%fused_computation.17 | output fusion | flops 10502271 | bytes 16777216 | tf_op jit(solution)/shard_map/div | solution.py:47
  51.1 1.9 slice_reduce_fusion
  53.1 3.1 %copy_convert_fusion = f32[8,128,1024]{2,0,1:T(8,128)} fusion(bf16[8,128,1024]{2,1,0:T(8,128)(2,1)S(1)} %copy-done.1), kind=kLoop, calls=%fused_computation.27 | loop fusion | flops 1048576 | bytes 6291456 | tf_op jit(solution)/shard_map/convert_element_type | solution.py:27
  56.2 3.9 %copy.40 = bf16[1024,1024]{0,1:T(8,128)(2,1)} copy(bf16[1024,1024]{1,0:T(8,128)(2,1)} %param.11) | data formatting | bytes 4194304 | tf_op args[4]
  60.1 9.0 %convolution_convert_fusion = bf16[8,128,16,64]{3,0,2,1:T(8,128)(2,1)} fusion(bf16[16,64,1024,1]{2,1,0,3:T(8,128)(2,1)} %bitcast.57, f32[1024]{0:T(1024)S(1)} %copy-done.7, f32[8,128]{0,1:T(8,128)S(1)} %add_rsqrt_fusion.2, f32[8,128]{0,1:T(8,128)S(1)} %broadcast_multiply_fusion, bf16[8,128,1024]{2,1,0:T(8,128)(2,1)} %param.7), kind=kOutput, calls=%fused_computation.18 | convolution fusion | flops 2153775104 | bytes 6303744 | tf_op jit(solution)/shard_map/dot_general | solution.py:38
  69.2 0.3 slice_reduce_fusion.1
  69.5 10.0 %fusion.2 = f32[8,16,1,64]{3,2,1,0:T(1,128)S(1)} fusion(f32[8,16,128,1]{2,3,1,0:T(1,128)S(1)} %bitcast.58, bf16[8,128,16,64]{3,0,2,1:T(8,128)(2,1)} %convolution_convert_fusion), kind=kOutput, calls=%fused_computation.6 | convolution fusion | flops 12582912 | bytes 2195456 | tf_op jit(solution)/shard_map/bhk,bkhd->bhd/dot_general | solution.py:50
  79.5 0.1 convert_element_type.55
  79.7 1.3 multiply_reduce_fusion.5
  81.0 43.4 %all_gather.3 = bf16[256,1024]{1,0:T(8,128)(2,1)S(1)} all-gather(bf16[8,1024]{1,0:T(8,128)(2,1)S(1)} %fusion.47), channel_id=1, replica_groups=mesh['dp'=32] {'dp'}, dimensions={0}, use_global_device_ids=true | all-gather | bytes 540672 | tf_op jit(solution)/shard_map/all_gather | solution.py:75
  124.4 0.4 exponential_reduce_fusion
  124.9 0.1 dynamic_slice.15
  125.0 0.4 multiply_reduce_fusion.3
  125.5 0.1 copy-done.5
  125.6 3.8 %fusion.25 = f32[1024,1024]{1,0:T(8,128)} fusion(bf16[8,1024]{1,0:T(8,128)(2,1)S(1)} %convert_element_type.55, f32[8,1024]{1,0:T(8,128)S(1)} %get-tuple-element.18, f32[8]{0:T(128)S(1)} %get-tuple-element.17, f32[8]{0:T(128)S(1)} %add_sqrt_fusion.1, f32[8,1024]{1,0:T(8,128)S(1)} %get-tuple-element.13), kind=kOutput, calls=%fused_computation.52 | convolution fusion | flops 100696064 | bytes 4276288 | tf_op jit(solution)/shard_map/dot_general | solution.py:102
  129.3 88.3 %all-reduce.1 = bf16[1024,1024]{1,0:T(8,128)(2,1)} all-reduce(f32[1024,1024]{1,0:T(8,128)} %fusion.25), channel_id=1, replica_groups=mesh['dp'=32] {'dp'}, use_global_device_ids=true, to_apply=%region_15.16 | all-reduce | flops 1048576 | bytes 6291456 | tf_op jit(solution)/shard_map/psum | solution.py:103
  217.6 1.0 multiply_reduce_fusion.4
  218.6 2.4 %gather_fusion = f32[256]{0:T(256)S(1)} fusion(f32[256,256]{0,1:T(8,128)S(1)} %get-tuple-element.14, s32[256]{0:T(256)S(1)} %bitcast.54), kind=kCustom, calls=%fused_computation | custom fusion | bytes 4096 | tf_op jit(solution)/shard_map/jit(diagonal)/cond/branch_0_fun/gather | solution.py:84
  221.0 0.7 subtract_reduce_fusion
  221.7 0.7 subtract_divide_fusion
  (28 shorter events, 0.4 us)
Async XLA Ops:
  0.6 79.0 %copy-start = (bf16[1024,1024]{1,0:T(8,128)(2,1)S(1)}, bf16[1024,1024]{1,0:T(8,128)(2,1)}, u32[]{:S(2)}) copy-start(bf16[1024,1024]{1,0:T(8,128)(2,1)} %param.12) | copy-start | bytes 6291460
  3.4 121.1 %all-to-all-start = ((bf16[32,8,1024]{2,1,0:T(8,128)(2,1)}), bf16[32,8,1024]{2,1,0:T(8,128)(2,1)S(1)}, u32[]{:S(2)}, u32[]{:S(2)}) async-start(bf16[32,8,1024]{2,1,0:T(8,128)(2,1)} %stack.2), calls=%async_computation | async-start | bytes 1048576 | tf_op jit(solution)/shard_map/all_to_all | solution.py:77
  16.4 7.9 %copy-start.7 = (f32[1024]{0:T(1024)S(1)}, f32[1024]{0:T(1024)}, u32[]{:S(2)}) copy-start(f32[1024]{0:T(1024)} %param.8) | copy-start | bytes 12292
  24.3 3.1 %copy-start.4 = (bf16[1024,1024]{0,1:T(8,128)(2,1)S(1)}, bf16[1024,1024]{0,1:T(8,128)(2,1)}, u32[]{:S(2)}) copy-start(bf16[1024,1024]{0,1:T(8,128)(2,1)} %copy.38) | copy-start | bytes 6291460
  27.4 3.5 %copy-start.3 = (bf16[1024,1024]{0,1:T(8,128)(2,1)S(1)}, bf16[1024,1024]{0,1:T(8,128)(2,1)}, u32[]{:S(2)}) copy-start(bf16[1024,1024]{0,1:T(8,128)(2,1)} %copy.36) | copy-start | bytes 6291460
  51.1 2.0 copy-start.1
  60.1 9.0 %copy-start.2 = (f32[8,128,1024]{2,0,1:T(8,128)S(1)}, f32[8,128,1024]{2,0,1:T(8,128)}, u32[]{:S(2)}) copy-start(f32[8,128,1024]{2,0,1:T(8,128)} %copy_convert_fusion) | copy-start | bytes 12582916
  124.9 0.7 copy-start.5
  129.3 88.3 %copy-start.6 = (bf16[8,1024]{1,0:T(8,128)(2,1)S(1)}, bf16[8,1024]{1,0:T(8,128)(2,1)}, u32[]{:S(2)}) copy-start(bf16[8,1024]{1,0:T(8,128)(2,1)} %param.13) | copy-start | bytes 49156
